TPU v7x, 32 devices: a whole 2x2x4 slice. The times are simulated.
32 devices in a mesh: seq: 8 (over z, y), head: 4 (over x, core).
Axes of the slice: x: 2, y: 2, z: 4, core: 2. Of those that a mesh axis runs over, the one named last changes fastest.
Arguments:
- queries: bfloat16 [2048, 4096], P('seq', 'head'), may hold values from -8 to 8
- self_keys: bfloat16 [2048, 1024], P('seq', 'head'), may hold values from -6 to 6
- self_values: bfloat16 [2048, 1024], P('seq', 'head'), may hold values from -6 to 6
- store_keys: bfloat16 [32768, 1024], P('seq', 'head'), may hold values from -6 to 6
- store_values: bfloat16 [32768, 1024], P('seq', 'head'), may hold values from -6 to 6
- kv_slot: int32 [256], replicated, may hold values from 0 to 255, as said below
- neighbours: int32 [16, 64], P('seq'), may hold values from 0 to 255, as said below
- counts: int32 [16], P('seq'), may hold values from 1 to 64, 96 in all
- out_weight: bfloat16 [4096, 4096], P('head', 'seq'), may hold values from -0.375 to 0.375
Outputs:
- mixed: bfloat16 [2048, 4096], P(('seq', 'head'))
Inputs may be any that keep to these rules, and one draw needn't show every extreme that they name: A permutation of the store blocks: block b is stored at slot kv_slot[b], on index kv_slot[b] // 32 of seq. `neighbours`: each row names 64 different store blocks in no particular order; only entries e < counts of the row are listed, the rest is padding. Counting by the index of seq on which a block is stored, each row names exactly 8 blocks on every index, and the 2 rows of one index of seq name the same single block on every index of seq.
All inputs are finite; a program needn't handle non-finite values. No bound on the sum of `counts` on one device may be relied on, other than what follows from the above.
Results may differ from a plain program's by a relative error of at most 0.012.
Values may be sent and summed in bfloat16 or wider, within the bound.
A program may use at most 128 MiB of HBM per device.

v0:
```python
import jax
import jax.numpy as jnp
from jax import lax
from jax.sharding import PartitionSpec as P

H = 32
KVH = 8
DH = 128
BLK = 128


def owner_ranks(slot_table, adjacency, store_blocks, per_owner):
    slot_ids = jnp.take(slot_table, adjacency, axis=0)
    owners = slot_ids // store_blocks
    local_index = slot_ids % store_blocks
    degree = adjacency.shape[-1]
    same_owner = owners[..., :, None] == owners[..., None, :]
    earlier = jnp.arange(degree)[None, :] < jnp.arange(degree)[:, None]
    ranking = jnp.sum(jnp.logical_and(same_owner, earlier), axis=-1)
    column = jnp.arange(adjacency.shape[1])[None, :, None] * per_owner + jnp.minimum(
        ranking, per_owner - 1
    )
    target = owners * (adjacency.shape[1] * per_owner) + column
    return (target, local_index)


def spread_table(target, values, columns_all):
    requesters = target.shape[0]
    onehot = target.reshape(requesters, -1)[:, :, None] == jnp.arange(columns_all)[None, None, :]
    spread = jnp.sum(jnp.where(onehot, values.reshape(requesters, -1)[:, :, None], 0), axis=1)
    filled = jnp.any(onehot, axis=1)
    return (spread, filled)


def unique_rows(wanted, capacity):
    length = wanted.shape[-1]
    equals = wanted[..., :, None] == wanted[..., None, :]
    earlier = jnp.arange(length)[None, :] < jnp.arange(length)[:, None]
    first_seen = jnp.logical_not(jnp.any(jnp.logical_and(equals, earlier), axis=-1))
    labels = jnp.cumsum(first_seen.astype(jnp.int32), axis=-1) - 1
    first_at = jnp.argmax(equals, axis=-1)
    mapping = jnp.take_along_axis(labels, first_at, axis=-1)
    chosen = jnp.logical_and(first_seen[..., :, None], labels[..., :, None] == jnp.arange(capacity))
    unique = jnp.sum(jnp.where(chosen, wanted[..., :, None], 0), axis=-2)
    return (unique, mapping)


def body(
    queries,
    self_keys,
    self_values,
    store_keys,
    store_values,
    kv_slot,
    neighbours,
    counts,
    out_weight,
):
    seq_count = lax.axis_size("seq")
    local_blocks, degree = neighbours.shape
    kv_width = store_keys.shape[1]
    kv_here = kv_width // DH
    store_blocks = store_keys.shape[0] // BLK
    per_owner = degree // seq_count
    per_device = min(store_blocks, max(per_owner, local_blocks * per_owner // 2))
    slot_width = local_blocks * per_owner
    per_group = H // KVH
    scaling = DH ** (-0.5)
    stored_keys = store_keys.reshape(store_blocks, BLK, kv_width)
    stored_values = store_values.reshape(store_blocks, BLK, kv_width)
    target, local_index = owner_ranks(kv_slot, neighbours[None], store_blocks, per_owner)
    wanted, filled = spread_table(target, local_index, seq_count * slot_width)
    wanted = wanted.reshape(-1, seq_count, slot_width)
    filled = filled.reshape(-1, seq_count, slot_width)
    spare_id = jnp.maximum(jnp.max(jnp.where(filled, wanted, -1), axis=-1, keepdims=True), 0)
    wanted = jnp.where(filled, wanted, spare_id)
    wanted, mapping = unique_rows(wanted, per_device)
    asked_for = lax.all_to_all(wanted[0], "seq", split_axis=0, concat_axis=0, tiled=True)
    sent_keys = jnp.take(stored_keys, asked_for, axis=0)
    sent_values = jnp.take(stored_values, asked_for, axis=0)
    got_keys = lax.all_to_all(sent_keys, "seq", split_axis=0, concat_axis=0, tiled=True)
    got_values = lax.all_to_all(sent_values, "seq", split_axis=0, concat_axis=0, tiled=True)
    own_target = target[0]
    own_map = mapping[0]
    query_blocks = queries.reshape(local_blocks, BLK, queries.shape[1])
    near_keys_all = self_keys.reshape(local_blocks, BLK, kv_width)
    near_values_all = self_values.reshape(local_blocks, BLK, kv_width)
    causal = jnp.arange(BLK)[:, None] >= jnp.arange(BLK)[None, :]
    is_live = (jnp.arange(degree)[None, :] < counts[:, None]).astype(jnp.int32)
    live_table, _ = spread_table(own_target[None], is_live[None], seq_count * slot_width)
    live_table = live_table.reshape(seq_count, slot_width) > 0

    def padded_block(block_index):
        query_rows = lax.dynamic_index_in_dim(query_blocks, block_index, 0, keepdims=False)
        near_keys = lax.dynamic_index_in_dim(near_keys_all, block_index, 0, keepdims=False)
        near_values = lax.dynamic_index_in_dim(near_values_all, block_index, 0, keepdims=False)
        live_part = lax.dynamic_slice_in_dim(live_table, block_index * per_owner, per_owner, 1)
        picked = lax.dynamic_slice_in_dim(own_map, block_index * per_owner, per_owner, 1)
        far_keys = jnp.take_along_axis(got_keys, picked[:, :, None, None], axis=1)
        far_values = jnp.take_along_axis(got_values, picked[:, :, None, None], axis=1)
        far_keys = far_keys.reshape(-1, kv_width)
        far_values = far_values.reshape(-1, kv_width)
        live_keys = jnp.broadcast_to(live_part[:, :, None], (seq_count, per_owner, BLK)).reshape(-1)
        pieces = []
        for kv_head in range(kv_here):
            query_group = query_rows[
                :, kv_head * per_group * DH : (kv_head + 1) * per_group * DH
            ].reshape(BLK, per_group, DH)
            key_cols = slice(kv_head * DH, (kv_head + 1) * DH)
            nearby = (
                jnp.einsum(
                    "trd,ud->rtu",
                    query_group,
                    near_keys[:, key_cols],
                    preferred_element_type=jnp.float32,
                )
                * scaling
            )
            nearby = jnp.where(causal[None], nearby, -jnp.inf)
            remote = (
                jnp.einsum(
                    "trd,kd->rtk",
                    query_group,
                    far_keys[:, key_cols],
                    preferred_element_type=jnp.float32,
                )
                * scaling
            )
            remote = jnp.where(live_keys[None, None, :], remote, -jnp.inf)
            highest = jnp.maximum(jnp.max(nearby, axis=-1), jnp.max(remote, axis=-1))
            near_weights = jnp.exp(nearby - highest[..., None])
            far_weights = jnp.exp(remote - highest[..., None])
            totals = jnp.sum(near_weights, axis=-1) + jnp.sum(far_weights, axis=-1)
            summed = jnp.einsum(
                "rtu,ud->rtd",
                near_weights.astype(jnp.bfloat16),
                near_values[:, key_cols],
                preferred_element_type=jnp.float32,
            )
            summed = summed + jnp.einsum(
                "rtk,kd->rtd",
                far_weights.astype(jnp.bfloat16),
                far_values[:, key_cols],
                preferred_element_type=jnp.float32,
            )
            pieces.append(
                jnp.transpose(summed / totals[..., None], (1, 0, 2)).reshape(BLK, per_group * DH)
            )
        return jnp.concatenate(pieces, axis=1).astype(jnp.bfloat16)

    attended = lax.map(padded_block, jnp.arange(local_blocks))
    attended = attended.reshape(local_blocks * BLK, -1)
    partial_value = jnp.dot(
        attended,
        lax.all_gather(out_weight, "seq", axis=1, tiled=True),
        preferred_element_type=jnp.float32,
    )
    return lax.psum_scatter(
        partial_value.astype(jnp.bfloat16), "head", scatter_dimension=0, tiled=True
    )


def solution(mesh):
    placed = (
        P("seq", "head"),
        P("seq", "head"),
        P("seq", "head"),
        P("seq", "head"),
        P("seq", "head"),
        P(),
        P("seq", None),
        P("seq"),
        P("head", "seq"),
    )
    return jax.shard_map(
        body, mesh=mesh, in_specs=placed, out_specs=P(("seq", "head"), None), check_vma=False
    )
```

profile of v0, /device:TPU:0, one launch (start us, length us, event | category | flops | bytes accessed | tf_op | source)
XLA Modules:
  0.0 492.7 jit_solution(13562793564419558064)
XLA Ops:
  12.7 13.6 %all_to_all.22 = s32[8,1,8]{2,1,0:T(1,128)S(1)} all-to-all(s32[8,1,8]{2,1,0:T(1,128)S(1)} %bitcast.244), channel_id=1, replica_groups=mesh['seq'=8,'head'=4] {'seq'}, dimensions={0} | all-to-all | bytes 512 | tf_op jit(solution)/shard_map/all_to_all | solution.py:78
  33.5 5.2 %broadcast_select_fusion.2 = (bf16[8,8,128,256]{3,2,1,0:T(8,128)(2,1)}, bf16[8,8,128,256]{3,2,1,0:T(8,128)(2,1)S(1)}) fusion(bf16[8,8,128,256]{3,2,1,0:T(8,128)(2,1)} %bitcast.229, pred[8,8]{1,0:T(8,128)(4,1)S(1)} %compare_and_fusion.1, bf16[8,8,128,256]{3,2,1,0:T(8,128)(2,1)} %bitcast.228), kind=kLoop, calls=%fused_computation.76 | loop fusion | flops 4194304 | bytes 16777280 | tf_op jit(solution)/shard_map/jit(_take)/select_n | solution.py:80
  38.7 95.5 %all_to_all.23 = bf16[8,8,128,256]{3,2,1,0:T(8,128)(2,1)} all-to-all(bf16[8,8,128,256]{3,2,1,0:T(8,128)(2,1)S(1)} %get-tuple-element.194), channel_id=1, replica_groups=mesh['seq'=8,'head'=4] {'seq'}, dimensions={0} | all-to-all | bytes 8388608 | tf_op jit(solution)/shard_map/all_to_all | solution.py:81
  134.2 4.6 all-to-all-start.2
  141.9 156.9 %all-to-all-done.2 = bf16[8,8,128,256]{3,2,1,0:T(8,128)(2,1)} async-done(((bf16[8,8,128,256]{3,2,1,0:T(8,128)(2,1)}), bf16[8,8,128,256]{3,2,1,0:T(8,128)(2,1)}, u32[]{:S(2)}, u32[]{:S(2)}) %all-to-all-start.2) | async-done | bytes 4194336 | tf_op jit(solution)/shard_map/all_to_all | solution.py:82
  298.8 151.1 %while.12 = (s32[]{:T(128)}, bf16[2,128,1024]{2,1,0:T(8,128)(2,1)S(1)}, s32[2]{0:T(128)S(1)}, bf16[2,128,256]{2,1,0:T(8,128)(2,1)S(1)}, bf16[2,128,1024]{2,1,0:T...) while((s32[]{:T(128)}, ...), condition=%wide.region_18.21_spmd.clone.clone, body=%wide.region_9.20_spmd.clone.clone.sunk | while | flops 4460395520 | bytes 351173664 | solution.py:151
  300.4 5.1 %gather_fusion = bf16[64,128,256]{2,1,0:T(8,128)(2,1)} fusion(bf16[8,8,128,256]{3,2,1,0:T(8,128)(2,1)} %get-tuple-element.319, s32[64]{0:T(128)S(1)} %reshape.789), kind=kCustom, calls=%fused_computation.1.clone.clone.1 | custom fusion | bytes 8389120 | tf_op jit(solution)/shard_map/while/body/eval_jaxpr/jit(take_along_axis)/gather | solution.py:99
  312.5 6.2 %bitcast_reduce_fusion.3 = (f32[4,128]{1,0:T(4,128)S(1)}, f32[8192,128,4]{1,0,2:T(8,128)S(1)}) fusion(pred[8192]{0:T(1024)(128)(4,1)S(1)} %broadcast_bitcast_fusion.2, bf16[128,4,128]{0,2,1:T(8,128)(2,1)S(1)} %bitcast.232, bf16[8192,256]{1,0:T(8,128)(2,1)} %bitcast.223), kind=kOutput, calls=%fused_computation.11.clone.1 | convolution fusion | flops 1086324224 | bytes 19015680 | tf_op jit(solution)/shard_map/while/body/eval_jaxpr/trd,kd->rtk/dot_general | solution.py:121
  319.0 12.1 %fusion.80 = (f32[4,128]{1,0:T(4,128)S(1)}, f32[4,128]{1,0:T(4,128)S(1)}, f32[8192,128,4]{1,0,2:T(8,128)}) fusion(f32[8192,128,4]{1,0,2:T(8,128)S(1)} %get-tuple-element.272, f32[4,128]{1,0:T(4,128)S(1)} %max.30, pred[8192]{0:T(1024)(128)(4,1)S(1)} %broadcast_bitcast_fusion.2, bf16[128,4,128]{0,2,1:T(8,128)(2,1)S(1)} %bitcast.230, ...), kind=kOutput, calls=%fused_computation.15.clone.1 | convolution fusion | flops 1103100928 | bytes 35796992 | tf_op jit(solution)/shard_map/while/body/eval_jaxpr/trd,kd->rtk/dot_general | solution.py:121
  331.1 5.0 %gather_fusion.1 = bf16[64,128,256]{2,1,0:T(8,128)(2,1)} fusion(bf16[8,8,128,256]{3,2,1,0:T(8,128)(2,1)} %get-tuple-element.321, s32[64]{0:T(128)S(1)} %reshape.789), kind=kCustom, calls=%fused_computation.3.clone.clone.1 | custom fusion | bytes 8389120 | tf_op jit(solution)/shard_map/while/body/eval_jaxpr/jit(take_along_axis)/gather | solution.py:100
  336.2 6.6 %copy.85 = bf16[8,8,128,256]{2,1,0,3:T(8,128)(2,1)} copy(bf16[8,8,128,256]{3,2,1,0:T(8,128)(2,1)} %bitcast.222) | data formatting | bytes 8388608 | tf_op jit(solution)/shard_map/while/body/eval_jaxpr/jit(take_along_axis)/gather | solution.py:100
  345.5 8.3 %copy.86 = bf16[32,8,64,128]{3,1,2,0:T(8,128)(2,1)S(1)} copy(bf16[32,8,64,128]{3,2,1,0:T(8,128)(2,1)S(1)} %bitcast.220) | data formatting | bytes 8388608 | tf_op jit(solution)/shard_map/while
  358.0 8.0 %fusion.84 = f32[4,128]{1,0:T(4,128)S(1)} fusion(f32[8192,128,4]{1,0,2:T(8,128)} %get-tuple-element.276, f32[4,128]{1,0:T(4,128)S(1)} %max.31, pred[8192]{0:T(1024)(128)(4,1)S(1)} %broadcast_bitcast_fusion.2), kind=kLoop, calls=%fused_computation.17.clone.1 | loop fusion | flops 16776704 | bytes 16789504 | tf_op jit(solution)/shard_map/while/body/eval_jaxpr/reduce_sum | solution.py:133
  366.1 8.0 %fusion.82 = f32[4,128,128]{1,2,0:T(8,128)S(1)} fusion(f32[8192,128,4]{1,0,2:T(8,128)} %get-tuple-element.276, f32[4,128]{1,0:T(4,128)S(1)} %max.31, pred[8192]{0:T(1024)(128)(4,1)S(1)} %broadcast_bitcast_fusion.2, bf16[8192,256]{0,1:T(8,128)(2,1)S(1)} %bitcast.226), kind=kOutput, calls=%fused_computation.19.clone.1 | convolution fusion | flops 1090519040 | bytes 19146752 | tf_op jit(solution)/shard_map/while/body/eval_jaxpr/rtk,kd->rtd/dot_general | solution.py:140
  375.9 5.0 %gather_fusion = bf16[64,128,256]{2,1,0:T(8,128)(2,1)} fusion(bf16[8,8,128,256]{3,2,1,0:T(8,128)(2,1)} %get-tuple-element.319, s32[64]{0:T(128)S(1)} %reshape.789), kind=kCustom, calls=%fused_computation.1.clone.clone.1 | custom fusion | bytes 8389120 | tf_op jit(solution)/shard_map/while/body/eval_jaxpr/jit(take_along_axis)/gather | solution.py:99
  387.9 6.2 %bitcast_reduce_fusion.3 = (f32[4,128]{1,0:T(4,128)S(1)}, f32[8192,128,4]{1,0,2:T(8,128)S(1)}) fusion(pred[8192]{0:T(1024)(128)(4,1)S(1)} %broadcast_bitcast_fusion.2, bf16[128,4,128]{0,2,1:T(8,128)(2,1)S(1)} %bitcast.232, bf16[8192,256]{1,0:T(8,128)(2,1)} %bitcast.223), kind=kOutput, calls=%fused_computation.11.clone.1 | convolution fusion | flops 1086324224 | bytes 19015680 | tf_op jit(solution)/shard_map/while/body/eval_jaxpr/trd,kd->rtk/dot_general | solution.py:121
  394.4 12.1 %fusion.80 = (f32[4,128]{1,0:T(4,128)S(1)}, f32[4,128]{1,0:T(4,128)S(1)}, f32[8192,128,4]{1,0,2:T(8,128)}) fusion(f32[8192,128,4]{1,0,2:T(8,128)S(1)} %get-tuple-element.272, f32[4,128]{1,0:T(4,128)S(1)} %max.30, pred[8192]{0:T(1024)(128)(4,1)S(1)} %broadcast_bitcast_fusion.2, bf16[128,4,128]{0,2,1:T(8,128)(2,1)S(1)} %bitcast.230, ...), kind=kOutput, calls=%fused_computation.15.clone.1 | convolution fusion | flops 1103100928 | bytes 35796992 | tf_op jit(solution)/shard_map/while/body/eval_jaxpr/trd,kd->rtk/dot_general | solution.py:121
  406.6 5.0 %gather_fusion.1 = bf16[64,128,256]{2,1,0:T(8,128)(2,1)} fusion(bf16[8,8,128,256]{3,2,1,0:T(8,128)(2,1)} %get-tuple-element.321, s32[64]{0:T(128)S(1)} %reshape.789), kind=kCustom, calls=%fused_computation.3.clone.clone.1 | custom fusion | bytes 8389120 | tf_op jit(solution)/shard_map/while/body/eval_jaxpr/jit(take_along_axis)/gather | solution.py:100
  411.6 6.6 %copy.85 = bf16[8,8,128,256]{2,1,0,3:T(8,128)(2,1)} copy(bf16[8,8,128,256]{3,2,1,0:T(8,128)(2,1)} %bitcast.222) | data formatting | bytes 8388608 | tf_op jit(solution)/shard_map/while/body/eval_jaxpr/jit(take_along_axis)/gather | solution.py:100
  421.0 8.3 %copy.86 = bf16[32,8,64,128]{3,1,2,0:T(8,128)(2,1)S(1)} copy(bf16[32,8,64,128]{3,2,1,0:T(8,128)(2,1)S(1)} %bitcast.220) | data formatting | bytes 8388608 | tf_op jit(solution)/shard_map/while
  433.4 8.0 %fusion.84 = f32[4,128]{1,0:T(4,128)S(1)} fusion(f32[8192,128,4]{1,0,2:T(8,128)} %get-tuple-element.276, f32[4,128]{1,0:T(4,128)S(1)} %max.31, pred[8192]{0:T(1024)(128)(4,1)S(1)} %broadcast_bitcast_fusion.2), kind=kLoop, calls=%fused_computation.17.clone.1 | loop fusion | flops 16776704 | bytes 16789504 | tf_op jit(solution)/shard_map/while/body/eval_jaxpr/reduce_sum | solution.py:133
  441.5 8.0 %fusion.82 = f32[4,128,128]{1,2,0:T(8,128)S(1)} fusion(f32[8192,128,4]{1,0,2:T(8,128)} %get-tuple-element.276, f32[4,128]{1,0:T(4,128)S(1)} %max.31, pred[8192]{0:T(1024)(128)(4,1)S(1)} %broadcast_bitcast_fusion.2, bf16[8192,256]{0,1:T(8,128)(2,1)S(1)} %bitcast.226), kind=kOutput, calls=%fused_computation.19.clone.1 | convolution fusion | flops 1090519040 | bytes 19146752 | tf_op jit(solution)/shard_map/while/body/eval_jaxpr/rtk,kd->rtd/dot_general | solution.py:140
  450.0 7.2 %convolution_convert_fusion = bf16[256,4096]{1,0:T(8,128)(2,1)} fusion(bf16[256,1024]{1,0:T(8,128)(2,1)S(1)} %bitcast.245, bf16[1024,4096]{1,0:T(8,128)(2,1)} %all-gather.2.cloned.1.call-done), kind=kOutput, calls=%fused_computation.75 | convolution fusion | flops 2148532224 | bytes 11010048 | tf_op jit(solution)/shard_map/dot_general | solution.py:153
  457.2 28.6 %reduce-scatter.2.cloned.1.call-done = bf16[64,4096]{1,0:T(8,128)(2,1)} async-done(((bf16[256,4096]{1,0:T(8,128)(2,1)}), bf16[64,4096]{1,0:T(8,128)(2,1)}) %reduce-scatter.2.cloned.1.call-update) | async-done | bytes 524304 | tf_op jit(solution)/shard_map/reduce_scatter | solution.py:158
  (141 shorter events, 43.1 us)
Async XLA Ops:
  6.5 19.8 %copy-start = (bf16[4096,256]{1,0:T(8,128)(2,1)S(1)}, bf16[4096,256]{1,0:T(8,128)(2,1)}, u32[]{:S(2)}) copy-start(bf16[4096,256]{1,0:T(8,128)(2,1)} %param.18) | copy-start | bytes 6291460
  134.2 164.6 %all-to-all-start.2 = ((bf16[8,8,128,256]{3,2,1,0:T(8,128)(2,1)}), bf16[8,8,128,256]{3,2,1,0:T(8,128)(2,1)}, u32[]{:S(2)}, u32[]{:S(2)}) async-start(bf16[8,8,128,256]{3,2,1,0:T(8,128)(2,1)} %get-tuple-element.193), calls=%async_computation.2 | async-start | bytes 8388608 | tf_op jit(solution)/shard_map/all_to_all | solution.py:82
  138.8 160.0 %copy-start.5 = (bf16[256,1024]{1,0:T(8,128)(2,1)S(1)}, bf16[256,1024]{1,0:T(8,128)(2,1)}, u32[]{:S(2)}) copy-start(bf16[256,1024]{1,0:T(8,128)(2,1)} %param.15) | copy-start | bytes 1572868
  138.8 160.0 %copy-start.6 = (bf16[256,256]{1,0:T(8,128)(2,1)S(1)}, bf16[256,256]{1,0:T(8,128)(2,1)}, u32[]{:S(2)}) copy-start(bf16[256,256]{1,0:T(8,128)(2,1)} %param.16) | copy-start | bytes 393220
  138.8 160.0 %copy-start.7 = (bf16[256,256]{1,0:T(8,128)(2,1)S(1)}, bf16[256,256]{1,0:T(8,128)(2,1)}, u32[]{:S(2)}) copy-start(bf16[256,256]{1,0:T(8,128)(2,1)} %param.17) | copy-start | bytes 393220
  138.8 311.1 %all-gather.2.cloned.1.call-start = ((), (), s32[]{:S(2)}) async-start(), calls=%async_computation.4 | async-start | bytes 9437184 | tf_op jit(solution)/shard_map/all_gather | solution.py:155
  139.6 346.2 %reduce-scatter.2.cloned.1.call-start = ((), (), s32[]{:S(2)}) async-start(), calls=%async_computation.5 | async-start | bytes 2621440 | tf_op jit(solution)/shard_map/reduce_scatter | solution.py:158
  312.5 6.5 %copy-start.2 = (bf16[8,8,128,256]{3,2,1,0:T(8,128)(2,1)S(1)}, bf16[8,8,128,256]{3,2,1,0:T(8,128)(2,1)}, u32[]{:S(2)}) copy-start(bf16[8,8,128,256]{3,2,1,0:T(8,128)(2,1)} %broadcast_select_fusion.9) | copy-start | bytes 12582916 | tf_op jit(solution)/shard_map/while
  318.7 12.3 %copy-start.8 = (f32[8192,128,4]{1,0,2:T(8,128)}, f32[8192,128,4]{1,0,2:T(8,128)S(1)}, u32[]{:S(2)}) copy-start(f32[8192,128,4]{1,0,2:T(8,128)S(1)} %get-tuple-element.272) | copy-start | bytes 50331652 | tf_op jit(solution)/shard_map/while
  342.7 11.2 %copy-start.9 = (f32[8192,128,4]{1,0,2:T(8,128)S(1)}, f32[8192,128,4]{1,0,2:T(8,128)}, u32[]{:S(2)}) copy-start(f32[8192,128,4]{1,0,2:T(8,128)} %copy-done.8) | copy-start | bytes 50331652 | tf_op jit(solution)/shard_map/while
  353.9 3.5 copy-start.3
  357.9 8.1 %copy-start.4 = (bf16[32,8,64,128]{3,1,2,0:T(8,128)(2,1)S(1)}, bf16[32,8,64,128]{3,1,2,0:T(8,128)(2,1)}, u32[]{:S(2)}) copy-start(bf16[32,8,64,128]{3,1,2,0:T(8,128)(2,1)} %copy-done.3) | copy-start | bytes 12582916 | tf_op jit(solution)/shard_map/while
  387.9 6.5 %copy-start.2 = (bf16[8,8,128,256]{3,2,1,0:T(8,128)(2,1)S(1)}, bf16[8,8,128,256]{3,2,1,0:T(8,128)(2,1)}, u32[]{:S(2)}) copy-start(bf16[8,8,128,256]{3,2,1,0:T(8,128)(2,1)} %broadcast_select_fusion.9) | copy-start | bytes 12582916 | tf_op jit(solution)/shard_map/while
  394.1 12.3 %copy-start.8 = (f32[8192,128,4]{1,0,2:T(8,128)}, f32[8192,128,4]{1,0,2:T(8,128)S(1)}, u32[]{:S(2)}) copy-start(f32[8192,128,4]{1,0,2:T(8,128)S(1)} %get-tuple-element.272) | copy-start | bytes 50331652 | tf_op jit(solution)/shard_map/while
  418.2 11.2 %copy-start.9 = (f32[8192,128,4]{1,0,2:T(8,128)S(1)}, f32[8192,128,4]{1,0,2:T(8,128)}, u32[]{:S(2)}) copy-start(f32[8192,128,4]{1,0,2:T(8,128)} %copy-done.8) | copy-start | bytes 50331652 | tf_op jit(solution)/shard_map/while
  429.3 3.5 copy-start.3
  433.4 8.1 %copy-start.4 = (bf16[32,8,64,128]{3,1,2,0:T(8,128)(2,1)S(1)}, bf16[32,8,64,128]{3,1,2,0:T(8,128)(2,1)}, u32[]{:S(2)}) copy-start(bf16[32,8,64,128]{3,1,2,0:T(8,128)(2,1)} %copy-done.3) | copy-start | bytes 12582916 | tf_op jit(solution)/shard_map/while
  450.0 35.9 %copy-start.1 = (bf16[4096,256]{1,0:T(8,128)(2,1)S(1)}, bf16[4096,256]{1,0:T(8,128)(2,1)}, u32[]{:S(2)}) copy-start(bf16[4096,256]{1,0:T(8,128)(2,1)} %param.18) | copy-start | bytes 6291460
Sparse Core Ops, SparseCore 0:
  141.7 193.3 all-gather.1
  457.4 28.4 reduce-scatter.1
where the time goes:
time: 494 us; the launch traced here: 493 us
  waiting for transfers between devices  186 us (38%)
  blocking collectives  109 us (22%)
  matrix products  68.3 us (14%)
  local copies, waits for them, and re-layouts  63.6 us (13%)
  other arithmetic  41.3 us (8%)
  between operations  13.6 us (3%)
  loops' own time  5.9 us (1%)
    all_to_all x1, waiting for transfers between devices, body(): lax.all_to_all(sent_values, 'seq', split_axis=0, concat_axis=0, tiled=True)  157 us
    all_to_all x1, blocking collectives, body(): lax.all_to_all(sent_keys, 'seq', split_axis=0, concat_axis=0, tiled=True)  95.5 us
    dot_general x4, matrix products, padded_block(): jnp.einsum('trd,kd->rtk', query_group, far_keys[:, key_cols], preferred_e...  36.6 us
    reduce_scatter x1, waiting for transfers between devices, body(): lax.psum_scatter(partial_value.astype(jnp.bfloat16), 'head', scatter_dime...  28.6 us
    gather x4, local copies, waits for them, and re-layouts, padded_block(): jnp.take_along_axis(got_values, picked[:, :, None, None], axis=1)  23.2 us
    dot_general x4, matrix products, padded_block(): jnp.einsum('rtk,kd->rtd', far_weights.astype(jnp.bfloat16), far_values[:,...  22.9 us
    while x22, local copies, waits for them, and re-layouts  16.7 us
    reduce_sum x6, other arithmetic, padded_block(): totals = jnp.sum(near_weights, axis=-1) + jnp.sum(far_weights, axis=-1)  16.3 us
  transfers between devices with their start and end apart: 3, of which 2 were waited for; matrix products, arithmetic and copies ran while one was open for 30% of the time, Pallas kernels for 0%

commit v1 on v0

v1 whole, which is shorter than its diff:
```python
import functools

import jax
import jax.numpy as jnp
from jax import lax
from jax.experimental import pallas as pl
from jax.experimental.pallas import tpu as pltpu
from jax.sharding import PartitionSpec as P

H = 32
KVH = 8
DH = 128
BLK = 128
NEG = -1e30
MESH = pl.DeviceIdType.MESH


def part_kernel(
    local_blocks,
    store_blocks,
    slot_ref,
    near_ref,
    count_ref,
    q_ref,
    sk_ref,
    sv_ref,
    k_ref,
    v_ref,
    o_ref,
    lse_ref,
    list_ref,
    acc_ref,
    max_ref,
    sum_ref,
):
    block = pl.program_id(0)
    me = lax.axis_index("seq")
    per_group = H // KVH
    kv_here = k_ref.shape[1] // DH
    rows = per_group * BLK
    scaling = DH ** (-0.5)

    def scan_entry(e, found):
        slot = slot_ref[near_ref[block, e]]
        list_ref[found] = lax.rem(slot, store_blocks)
        return found + (slot // store_blocks == me).astype(jnp.int32)

    found = lax.fori_loop(0, count_ref[block], scan_entry, jnp.int32(0))
    home = block // local_blocks == me

    @pl.when(jnp.logical_and(found == 0, jnp.logical_not(home)))
    def _():
        o_ref[...] = jnp.zeros_like(o_ref)
        lse_ref[...] = jnp.full_like(lse_ref, NEG)

    @pl.when(jnp.logical_or(found > 0, home))
    def _():
        def group_queries(g):
            return jnp.concatenate(
                [q_ref[:, (g * per_group + r) * DH : (g * per_group + r + 1) * DH] for r in range(per_group)],
                axis=0,
            )

        def scores_of(g, keys):
            return (
                lax.dot_general(
                    group_queries(g), keys, (((1,), (1,)), ((), ())), preferred_element_type=jnp.float32
                )
                * scaling
            )

        @pl.when(home)
        def _():
            start = pl.multiple_of(lax.rem(block, local_blocks) * BLK, BLK)
            position = lax.rem(lax.broadcasted_iota(jnp.int32, (rows, BLK), 0), BLK)
            causal = position >= lax.broadcasted_iota(jnp.int32, (rows, BLK), 1)
            for g in range(kv_here):
                cols = slice(g * DH, (g + 1) * DH)
                s = jnp.where(causal, scores_of(g, sk_ref[pl.ds(start, BLK), cols]), NEG)
                m = jnp.max(s, axis=-1, keepdims=True)
                p = jnp.exp(s - m)
                max_ref[g] = jnp.broadcast_to(m, (rows, BLK))
                sum_ref[g] = jnp.broadcast_to(jnp.sum(p, axis=-1, keepdims=True), (rows, BLK))
                acc_ref[g] = jnp.dot(
                    p.astype(jnp.bfloat16), sv_ref[pl.ds(start, BLK), cols], preferred_element_type=jnp.float32
                )

        @pl.when(jnp.logical_not(home))
        def _():
            max_ref[...] = jnp.full_like(max_ref, NEG)
            sum_ref[...] = jnp.zeros_like(sum_ref)
            acc_ref[...] = jnp.zeros_like(acc_ref)

        @pl.loop(0, found)
        def _(i):
            start = pl.multiple_of(list_ref[i] * BLK, BLK)
            for g in range(kv_here):
                cols = slice(g * DH, (g + 1) * DH)
                s = scores_of(g, k_ref[pl.ds(start, BLK), cols])
                old = max_ref[g]
                new = jnp.maximum(old, jnp.max(s, axis=-1, keepdims=True))
                p = jnp.exp(s - new)
                shrink = jnp.exp(old - new)
                max_ref[g] = new
                sum_ref[g] = sum_ref[g] * shrink + jnp.sum(p, axis=-1, keepdims=True)
                acc_ref[g] = acc_ref[g] * shrink + jnp.dot(
                    p.astype(jnp.bfloat16), v_ref[pl.ds(start, BLK), cols], preferred_element_type=jnp.float32
                )

        lane = lax.broadcasted_iota(jnp.int32, (BLK, BLK), 1)
        tile = jnp.full((BLK, BLK), NEG, jnp.float32)
        for g in range(kv_here):
            total = sum_ref[g]
            normal = (acc_ref[g] / total).astype(jnp.bfloat16)
            lse = max_ref[g] + jnp.log(total)
            for r in range(per_group):
                h = g * per_group + r
                o_ref[:, h * DH : (h + 1) * DH] = normal[r * BLK : (r + 1) * BLK]
                tile = jnp.where(lane == h, lse[r * BLK : (r + 1) * BLK], tile)
        lse_ref[...] = jnp.transpose(tile)[: lse_ref.shape[0]]


def return_kernel(n, heads, o_ref, lse_ref, out_ref, got, got_lse, send_sem, recv_sem, lsend_sem, lrecv_sem, own_sem):
    me = lax.axis_index("seq")
    rows = out_ref.shape[0]
    srows = got_lse.shape[1]
    blocks = rows // BLK
    barrier = pltpu.get_barrier_semaphore()
    for k in range(1, n):
        pl.semaphore_signal(barrier, inc=1, device_id={"seq": lax.rem(me + k, n)}, device_id_type=MESH)
    own = pltpu.make_async_copy(o_ref.at[pl.ds(pl.multiple_of(me * rows, rows), rows)], got.at[0], own_sem.at[0])
    own.start()
    own_lse = pltpu.make_async_copy(
        lse_ref.at[pl.ds(pl.multiple_of(me * srows, srows), srows)], got_lse.at[0], own_sem.at[1]
    )
    own_lse.start()
    pl.semaphore_wait(barrier, n - 1)
    copies = []
    for k in range(1, n):
        to = lax.rem(me + k, n)
        copies.append(
            pltpu.make_async_remote_copy(
                src_ref=lse_ref.at[pl.ds(pl.multiple_of(to * srows, srows), srows)],
                dst_ref=got_lse.at[k],
                send_sem=lsend_sem.at[k],
                recv_sem=lrecv_sem.at[k],
                device_id={"seq": to},
                device_id_type=MESH,
            )
        )
        copies.append(
            pltpu.make_async_remote_copy(
                src_ref=o_ref.at[pl.ds(pl.multiple_of(to * rows, rows), rows)],
                dst_ref=got.at[k],
                send_sem=send_sem.at[k],
                recv_sem=recv_sem.at[k],
                device_id={"seq": to},
                device_id_type=MESH,
            )
        )
    for copy in copies:
        copy.start()
    own.wait()
    own_lse.wait()
    for copy in copies:
        copy.wait()
    for b in range(blocks):
        at = slice(b * heads, (b + 1) * heads)

        def peak(i, top):
            return jnp.maximum(top, got_lse[i, at])

        top = lax.fori_loop(1, n, peak, got_lse[0, at])

        def total_of(i, total):
            return total + jnp.exp(got_lse[i, at] - top)

        total = lax.fori_loop(1, n, total_of, jnp.exp(got_lse[0, at] - top))

        def share(i):
            part = jnp.exp(got_lse[i, at] - top) / total
            padded = jnp.concatenate([part, jnp.zeros((BLK - heads, BLK), jnp.float32)], axis=0)
            return jnp.transpose(padded)

        lines = slice(b * BLK, (b + 1) * BLK)

        def add(i, sums):
            weight = share(i)
            return tuple(
                sums[h]
                + got[i, lines, h * DH : (h + 1) * DH].astype(jnp.float32)
                * jnp.broadcast_to(weight[:, h : h + 1], (BLK, DH))
                for h in range(heads)
            )

        sums = lax.fori_loop(0, n, add, tuple(jnp.zeros((BLK, DH), jnp.float32) for _ in range(heads)))
        for h in range(heads):
            out_ref[lines, h * DH : (h + 1) * DH] = sums[h].astype(jnp.bfloat16)


def body(
    queries,
    self_keys,
    self_values,
    store_keys,
    store_values,
    kv_slot,
    neighbours,
    counts,
    out_weight,
):
    n = lax.axis_size("seq")
    local_blocks, degree = neighbours.shape
    width = queries.shape[1]
    heads = width // DH
    store_blocks = store_keys.shape[0] // BLK
    all_blocks = local_blocks * n
    kv_here = store_keys.shape[1] // DH
    rows = (H // KVH) * BLK
    lists = jnp.concatenate([neighbours, counts[:, None]], axis=1)
    lists = lax.all_gather(lists, "seq", axis=0, tiled=True)
    all_queries = lax.all_gather(queries, "seq", axis=0, tiled=True)
    weight = lax.all_gather(out_weight, "seq", axis=1, tiled=True)
    smem = pl.BlockSpec(memory_space=pltpu.SMEM)

    def whole(a):
        return pl.BlockSpec(a.shape, lambda i: (0, 0))

    parts, lse = pl.pallas_call(
        functools.partial(part_kernel, local_blocks, store_blocks),
        grid=(all_blocks,),
        in_specs=[smem, smem, smem, pl.BlockSpec((BLK, width), lambda i: (i, 0))]
        + [whole(a) for a in (self_keys, self_values, store_keys, store_values)],
        out_specs=[
            pl.BlockSpec((BLK, width), lambda i: (i, 0)),
            pl.BlockSpec((heads, BLK), lambda i: (i, 0)),
        ],
        out_shape=[
            jax.ShapeDtypeStruct((all_blocks * BLK, width), jnp.bfloat16),
            jax.ShapeDtypeStruct((all_blocks * heads, BLK), jnp.float32),
        ],
        scratch_shapes=[
            pltpu.SMEM((degree + 1,), jnp.int32),
            pltpu.VMEM((kv_here, rows, DH), jnp.float32),
            pltpu.VMEM((kv_here, rows, BLK), jnp.float32),
            pltpu.VMEM((kv_here, rows, BLK), jnp.float32),
        ],
        compiler_params=pltpu.CompilerParams(vmem_limit_bytes=40 << 20),
        cost_estimate=pl.CostEstimate(flops=2_000_000_000, bytes_accessed=12 << 20, transcendentals=4_000_000),
    )(
        kv_slot,
        lists[:, :degree],
        lists[:, degree],
        all_queries,
        self_keys,
        self_values,
        store_keys,
        store_values,
    )
    local_rows = queries.shape[0]
    attended = pl.pallas_call(
        functools.partial(return_kernel, n, heads),
        in_specs=[pl.BlockSpec(memory_space=pl.ANY)] * 2,
        out_specs=pl.BlockSpec(memory_space=pltpu.VMEM),
        out_shape=jax.ShapeDtypeStruct((local_rows, width), jnp.bfloat16),
        scratch_shapes=[
            pltpu.VMEM((n, local_rows, width), jnp.bfloat16),
            pltpu.VMEM((n, local_blocks * heads, BLK), jnp.float32),
            pltpu.SemaphoreType.DMA((n,)),
            pltpu.SemaphoreType.DMA((n,)),
            pltpu.SemaphoreType.DMA((n,)),
            pltpu.SemaphoreType.DMA((n,)),
            pltpu.SemaphoreType.DMA((2,)),
        ],
        compiler_params=pltpu.CompilerParams(
            collective_id=0, has_side_effects=True, vmem_limit_bytes=50 << 20
        ),
        cost_estimate=pl.CostEstimate(flops=80_000_000, bytes_accessed=80 << 20, transcendentals=0),
    )(parts, lse)
    partial_value = jnp.dot(attended, weight, preferred_element_type=jnp.float32)
    return lax.psum_scatter(
        partial_value.astype(jnp.bfloat16), "head", scatter_dimension=0, tiled=True
    )


def solution(mesh):
    placed = (
        P("seq", "head"),
        P("seq", "head"),
        P("seq", "head"),
        P("seq", "head"),
        P("seq", "head"),
        P(),
        P("seq", None),
        P("seq"),
        P("head", "seq"),
    )
    return jax.shard_map(
        body, mesh=mesh, in_specs=placed, out_specs=P(("seq", "head"), None), check_vma=False
    )
```

time: 494 us -> 338 us (0.68)
  Pallas kernels: 0 us -> 117 us
  blocking collectives: 109 us -> 22.6 us
  matrix products: 68.3 us -> 7.09 us
  local copies, waits for them, and re-layouts: 63.6 us -> 10.7 us
  other arithmetic: 41.3 us -> 0.75 us
  waiting for transfers between devices: 186 us -> 166 us
  loops' own time: 5.9 us -> 0 us
    all_to_all x1 -> x0, waiting for transfers between devices: 157 us -> none  [body(): lax.all_to_all(sent_values, 'seq', split_axis=0, concat_axis=0, tiled=True)]
    all_gather x1 -> x2, waiting for transfers between devices: 0.02 us -> 134 us  [the longest x1 81.5 us: body(): weight = lax.all_gather(out_weight, 'seq', axis=1, tiled=True)]
    pallas_call x0 -> x2, Pallas kernels: none -> 117 us  [the longest x1 102 us: body(): pl.pallas_call(functools.partial(return_kernel, n, heads), in_specs=[pl.B...]
    all_to_all x2 -> x0, blocking collectives: 109 us -> none  [the longest x1 95.5 us: body(): lax.all_to_all(sent_keys, 'seq', split_axis=0, concat_axis=0, tiled=True)]
    dot_general x17 -> x1, matrix products: 68.3 us -> 7.09 us  [body(): jnp.dot(attended, weight, preferred_element_type=jnp.float32)]
    gather x15 -> x0, local copies, waits for them, and re-layouts: 43.5 us -> none  [the longest x4 23.2 us: padded_block(): jnp.take_along_axis(got_values, picked[:, :, None, None], axis=1)]
    all_gather x0 -> x1, blocking collectives: none -> 22.6 us  [body(): lists = lax.all_gather(lists, 'seq', axis=0, tiled=True)]
    select_n x10 -> x0, other arithmetic: 21.5 us -> none  [the longest x2 9.1 us: padded_block(): far_keys = jnp.take_along_axis(got_keys, picked[:, :, None, None], axis=1)]
  transfers between devices with their start and end apart: 3 -> 3, of which waited for: 2 -> 3; matrix products, arithmetic and copies ran while one was open for 30% -> 0% of each run, Pallas kernels for 0% -> 35%
where the time goes in v1:
time: 338 us; the launch traced here: 337 us
  waiting for transfers between devices  166 us (49%)
  Pallas kernels  117 us (35%)
  blocking collectives  22.6 us (7%)
  between operations  13.1 us (4%)
  local copies, waits for them, and re-layouts  10.7 us (3%)
  matrix products  7.09 us (2%)
    pallas_call x1, Pallas kernels, body(): pl.pallas_call(functools.partial(return_kernel, n, heads), in_specs=[pl.B...  102 us
    all_gather x1, waiting for transfers between devices, body(): weight = lax.all_gather(out_weight, 'seq', axis=1, tiled=True)  81.5 us
    all_gather x1, waiting for transfers between devices, body(): all_queries = lax.all_gather(queries, 'seq', axis=0, tiled=True)  52.7 us
    reduce_scatter x1, waiting for transfers between devices, body(): lax.psum_scatter(partial_value.astype(jnp.bfloat16), 'head', scatter_dime...  30.5 us
    all_gather x1, blocking collectives, body(): lists = lax.all_gather(lists, 'seq', axis=0, tiled=True)  22.6 us
    pallas_call x1, Pallas kernels, body(): pl.pallas_call(functools.partial(part_kernel, local_blocks, store_blocks)...  14.7 us
    unnamed x14, local copies, waits for them, and re-layouts  9.81 us
    dot_general x1, matrix products, body(): jnp.dot(attended, weight, preferred_element_type=jnp.float32)  7.09 us
  transfers between devices with their start and end apart: 3, of which 3 were waited for; matrix products, arithmetic and copies ran while one was open for 0% of the time, Pallas kernels for 35%

profile of v1, /device:TPU:0, one launch (start us, length us, event | category | flops | bytes accessed | tf_op | source)
XLA Modules:
  0.0 337.5 jit_solution(11519008694598352479)
XLA Ops:
  6.5 0.0 all-gather.4.cloned.1.call-start
  6.5 0.7 all-gather.4.cloned.1.call-update
  7.3 0.0 all-gather.6.cloned.1.call-start
  7.3 0.7 all-gather.6.cloned.1.call-update
  8.0 0.0 reduce-scatter.2.cloned.1.call-start
  8.1 0.7 copy.12
  8.8 0.8 add_bitcast_fusion
  9.5 22.6 %all-gather = s32[8,2,65]{2,1,0:T(2,128)S(1)} all-gather(s32[1,2,65]{2,1,0:T(2,128)S(1)} %add_bitcast_fusion), channel_id=1, replica_groups=mesh['seq'=8,'head'=4] {'seq'}, dimensions={0}, use_global_device_ids=true | all-gather | bytes 4680 | tf_op jit(solution)/shard_map/all_gather | solution.py:221
  32.2 0.2 slice_reduce_fusion.count_ref
  32.3 52.7 %all-gather.4.cloned.1.call-done.q_ref = bf16[2048,1024]{1,0:T(8,128)(2,1)} async-done(((bf16[256,1024]{1,0:T(8,128)(2,1)}), bf16[2048,1024]{1,0:T(8,128)(2,1)}) %all-gather.4.cloned.1.call-update) | async-done | bytes 4194320 | tf_op jit(solution)/shard_map/all_gather | solution.py:222
  85.0 2.2 copy-done.1
  87.2 1.6 copy-done.2
  88.8 1.6 copy-done.3
  90.4 0.9 copy-done.4
  91.3 0.9 copy-done.5
  92.2 0.7 copy-done.6
  92.9 14.7 %shard_map.91 = (bf16[2048,1024]{1,0:T(8,128)(2,1)S(1)}, f32[128,128]{1,0:T(8,128)S(1)}) custom-call(s32[256]{0:T(256)S(1)} %copy-done.6, s32[16,64]{1,0:T(8,128)S(1)} %bitcast.8, s32[16]{0:T(128)S(1)} %slice_reduce_fusion.count_ref, bf16[2048,1024]{1,0:T(8,128)(2,1)S(1)} %copy-done.1, bf16[256,256]{1,0:T(8,128)(2,1)S(1)} %copy-done.4, ...), custom_call_target="tpu_custom_call" | custom-call | flops 2000000000 | bytes 12582912 | tf_op jit(solution)/shard_map/pallas_call | solution.py:229
  107.6 0.0 copy-start
  107.6 2.0 copy-done
  109.6 102.2 %shard_map.92 = bf16[256,1024]{1,0:T(8,128)(2,1)S(1)} custom-call(bf16[2048,1024]{1,0:T(8,128)(2,1)} %copy-done, f32[128,128]{1,0:T(8,128)S(1)} %get-tuple-element.8.lse_ref), custom_call_target="tpu_custom_call" | custom-call | flops 80000000 | bytes 83886080 | tf_op jit(solution)/shard_map/pallas_call | solution.py:261
  211.8 81.5 %all-gather.6.cloned.1.call-done = bf16[1024,4096]{1,0:T(8,128)(2,1)} async-done(((bf16[1024,512]{1,0:T(8,128)(2,1)}), bf16[1024,4096]{1,0:T(8,128)(2,1)}) %all-gather.6.cloned.1.call-update) | async-done | bytes 8388624 | tf_op jit(solution)/shard_map/all_gather | solution.py:223
  293.4 7.1 %convolution_convert_fusion = bf16[256,4096]{1,0:T(8,128)(2,1)} fusion(bf16[256,1024]{1,0:T(8,128)(2,1)S(1)} %shard_map.92, bf16[1024,4096]{1,0:T(8,128)(2,1)} %all-gather.6.cloned.1.call-done), kind=kOutput, calls=%fused_computation | convolution fusion | flops 2148532224 | bytes 11010048 | tf_op jit(solution)/shard_map/dot_general | solution.py:280
  300.5 0.0 reduce-scatter.2.cloned.1.call-update
  300.5 30.5 %reduce-scatter.2.cloned.1.call-done = bf16[64,4096]{1,0:T(8,128)(2,1)} async-done(((bf16[256,4096]{1,0:T(8,128)(2,1)}), bf16[64,4096]{1,0:T(8,128)(2,1)}) %reduce-scatter.2.cloned.1.call-update) | async-done | bytes 524304 | tf_op jit(solution)/shard_map/reduce_scatter | solution.py:281
  (6 shorter events, 0.0 us)
Async XLA Ops:
  6.5 78.5 %all-gather.4.cloned.1.call-start = ((), (), s32[]{:S(2)}) async-start(), calls=%async_computation.1 | async-start | bytes 4718592 | tf_op jit(solution)/shard_map/all_gather | solution.py:222
  7.3 286.1 %all-gather.6.cloned.1.call-start = ((), (), s32[]{:S(2)}) async-start(), calls=%async_computation.2 | async-start | bytes 9437184 | tf_op jit(solution)/shard_map/all_gather | solution.py:223
  8.0 323.0 %reduce-scatter.2.cloned.1.call-start = ((), (), s32[]{:S(2)}) async-start(), calls=%async_computation.3 | async-start | bytes 2621440 | tf_op jit(solution)/shard_map/reduce_scatter | solution.py:281
  85.0 2.2 copy-start.1
  87.2 1.6 copy-start.2
  88.8 1.6 copy-start.3
  90.4 0.9 copy-start.4
  91.3 0.9 copy-start.5
  92.2 0.7 copy-start.6
  107.6 2.0 copy-start
Sparse Core Ops, SparseCore 0:
  9.5 75.5 all-gather.3
  87.1 206.2 all-gather.5
  300.6 30.2 reduce-scatter.1

commit v2 on v1

v2 whole, which is shorter than its diff:
```python
import functools

import jax
import jax.numpy as jnp
from jax import lax
from jax.experimental import pallas as pl
from jax.experimental.pallas import tpu as pltpu
from jax.sharding import PartitionSpec as P

H = 32
KVH = 8
DH = 128
BLK = 128
NEG = -1e30
STAT = 8
MESH = pl.DeviceIdType.MESH


def part_kernel(
    local_blocks,
    store_blocks,
    slot_ref,
    near_ref,
    count_ref,
    q_ref,
    sk_ref,
    sv_ref,
    k_ref,
    v_ref,
    o_ref,
    lse_ref,
    list_ref,
    acc_ref,
    max_ref,
    sum_ref,
):
    block = pl.program_id(0)
    me = lax.axis_index("seq")
    per_group = H // KVH
    kv_here = k_ref.shape[1] // DH
    rows = per_group * BLK
    scaling = DH ** (-0.5)

    def scan_entry(e, found):
        slot = slot_ref[near_ref[block, e]]
        list_ref[found] = lax.rem(slot, store_blocks)
        return found + (slot // store_blocks == me).astype(jnp.int32)

    found = lax.fori_loop(0, count_ref[block], scan_entry, jnp.int32(0))
    home = block // local_blocks == me

    @pl.when(jnp.logical_and(found == 0, jnp.logical_not(home)))
    def _():
        o_ref[...] = jnp.zeros_like(o_ref)
        lse_ref[...] = jnp.full_like(lse_ref, NEG)

    @pl.when(jnp.logical_or(found > 0, home))
    def _():
        def group_queries(g):
            return jnp.concatenate(
                [q_ref[:, (g * per_group + r) * DH : (g * per_group + r + 1) * DH] for r in range(per_group)],
                axis=0,
            )

        def scores_of(g, keys):
            return (
                lax.dot_general(
                    group_queries(g), keys, (((1,), (1,)), ((), ())), preferred_element_type=jnp.float32
                )
                * scaling
            )

        @pl.when(home)
        def _():
            start = pl.multiple_of(lax.rem(block, local_blocks) * BLK, BLK)
            position = lax.rem(lax.broadcasted_iota(jnp.int32, (rows, BLK), 0), BLK)
            causal = position >= lax.broadcasted_iota(jnp.int32, (rows, BLK), 1)
            for g in range(kv_here):
                cols = slice(g * DH, (g + 1) * DH)
                s = jnp.where(causal, scores_of(g, sk_ref[pl.ds(start, BLK), cols]), NEG)
                m = jnp.max(s, axis=-1, keepdims=True)
                p = jnp.exp(s - m)
                max_ref[g] = jnp.broadcast_to(m, (rows, BLK))
                sum_ref[g] = jnp.broadcast_to(jnp.sum(p, axis=-1, keepdims=True), (rows, BLK))
                acc_ref[g] = jnp.dot(
                    p.astype(jnp.bfloat16), sv_ref[pl.ds(start, BLK), cols], preferred_element_type=jnp.float32
                )

        @pl.when(jnp.logical_not(home))
        def _():
            max_ref[...] = jnp.full_like(max_ref, NEG)
            sum_ref[...] = jnp.zeros_like(sum_ref)
            acc_ref[...] = jnp.zeros_like(acc_ref)

        @pl.loop(0, found)
        def _(i):
            start = pl.multiple_of(list_ref[i] * BLK, BLK)
            for g in range(kv_here):
                cols = slice(g * DH, (g + 1) * DH)
                s = scores_of(g, k_ref[pl.ds(start, BLK), cols])
                old = max_ref[g]
                new = jnp.maximum(old, jnp.max(s, axis=-1, keepdims=True))
                p = jnp.exp(s - new)
                shrink = jnp.exp(old - new)
                max_ref[g] = new
                sum_ref[g] = sum_ref[g] * shrink + jnp.sum(p, axis=-1, keepdims=True)
                acc_ref[g] = acc_ref[g] * shrink + jnp.dot(
                    p.astype(jnp.bfloat16), v_ref[pl.ds(start, BLK), cols], preferred_element_type=jnp.float32
                )

        lane = lax.broadcasted_iota(jnp.int32, (BLK, BLK), 1)
        for g in range(kv_here):
            total = sum_ref[g]
            normal = (acc_ref[g] / total).astype(jnp.bfloat16)
            lse = max_ref[g] + jnp.log(total)
            tile = jnp.full((BLK, BLK), NEG, jnp.float32)
            for r in range(per_group):
                o_ref[0, g, :, r * DH : (r + 1) * DH] = normal[r * BLK : (r + 1) * BLK]
                tile = jnp.where(lane == r, lse[r * BLK : (r + 1) * BLK], tile)
            lse_ref[0, g] = jnp.transpose(tile)[:STAT]


def ring_place(index, n):
    odd = lax.rem(index, 2)
    half = index // 2
    return (1 - odd) * half + odd * (n - 1 - half)


def ring_index(place, n):
    place = lax.rem(place + 2 * n, n)
    far = place // (n // 2)
    return (1 - far) * (2 * place) + far * (2 * (n - 1 - place) + 1)


def gather_kernel(n, pieces, with_table, *refs):
    if with_table:
        x_ref, table_ref, out_ref, tables_ref, own_sem, send_sem, recv_sem, tsend_sem, trecv_sem = refs
    else:
        x_ref, out_ref, own_sem, send_sem, recv_sem = refs
    me = lax.axis_index("seq")
    place = ring_place(me, n)
    rows = x_ref.shape[0]
    sub = rows // pieces
    half = n // 2
    ways = (1, -1)
    beside = [ring_index(place + way, n) for way in ways]
    barrier = pltpu.get_barrier_semaphore()
    if with_table:
        for k in range(1, n):
            pl.semaphore_signal(barrier, inc=1, device_id={"seq": lax.rem(me + k, n)}, device_id_type=MESH)
    else:
        for other in beside:
            pl.semaphore_signal(barrier, inc=1, device_id={"seq": other}, device_id_type=MESH)
    own = pltpu.make_async_copy(x_ref, out_ref.at[pl.ds(pl.multiple_of(me * rows, rows), rows)], own_sem.at[0])
    own.start()
    pl.semaphore_wait(barrier, n - 1 if with_table else 2)

    def copy(way, step, piece):
        owner = ring_index(place - ways[way] * step, n)
        there = pl.ds(pl.multiple_of(owner * rows + piece * sub, sub), sub)
        source = x_ref.at[pl.ds(piece * sub, sub)] if step == 0 else out_ref.at[there]
        return pltpu.make_async_remote_copy(
            src_ref=source,
            dst_ref=out_ref.at[there],
            send_sem=send_sem.at[way, step, piece],
            recv_sem=recv_sem.at[way, step, piece],
            device_id={"seq": beside[way]},
            device_id_type=MESH,
        )

    table_copies = []
    if with_table:
        tables_ref[pl.ds(me, 1)] = table_ref[...][None]
        for k in range(1, n):
            table_copies.append(
                pltpu.make_async_remote_copy(
                    src_ref=table_ref,
                    dst_ref=tables_ref.at[me],
                    send_sem=tsend_sem.at[k],
                    recv_sem=trecv_sem.at[k],
                    device_id={"seq": lax.rem(me + k, n)},
                    device_id_type=MESH,
                )
            )
        for one in table_copies:
            one.start()
    started = []
    for step in range(half):
        for spot in range(pieces):
            for way in range(2):
                piece = spot if way == 0 else pieces - 1 - spot
                if step > 0:
                    copy(way, step - 1, piece).wait_recv()
                if step < half - 1 or spot < pieces // 2:
                    one = copy(way, step, piece)
                    one.start()
                    started.append(one)
    for spot in range(pieces // 2):
        for way in range(2):
            copy(way, half - 1, spot if way == 0 else pieces - 1 - spot).wait_recv()
    for one in started:
        one.wait_send()
    for one in table_copies:
        one.wait()
    own.wait()


def gathered(x, n, pieces, number, table=None):
    rows, width = x.shape
    with_table = table is not None
    vmem = pl.BlockSpec(memory_space=pltpu.VMEM)
    out_shape = [jax.ShapeDtypeStruct((n * rows, width), x.dtype)]
    scratch = [
        pltpu.SemaphoreType.DMA((1,)),
        pltpu.SemaphoreType.DMA((2, n // 2, pieces)),
        pltpu.SemaphoreType.DMA((2, n // 2, pieces)),
    ]
    if with_table:
        out_shape.append(jax.ShapeDtypeStruct((n,) + table.shape, table.dtype))
        scratch += [pltpu.SemaphoreType.DMA((n,)), pltpu.SemaphoreType.DMA((n,))]
    return pl.pallas_call(
        functools.partial(gather_kernel, n, pieces, with_table),
        in_specs=[vmem] * (1 + with_table),
        out_specs=[vmem] * (1 + with_table),
        out_shape=out_shape,
        scratch_shapes=scratch,
        compiler_params=pltpu.CompilerParams(
            collective_id=number, has_side_effects=True, vmem_limit_bytes=50 << 20
        ),
    )(*([x, table] if with_table else [x]))


def merge(lse_a, lse_b):
    top = jnp.maximum(lse_a, lse_b)
    a = jnp.exp(lse_a - top)
    b = jnp.exp(lse_b - top)
    total = a + b
    both = jnp.concatenate([a / total, b / total, jnp.zeros((BLK - 2 * STAT, BLK), jnp.float32)], axis=0)
    return jnp.transpose(both), top + jnp.log(total)


def reduce_kernel(n, o_ref, lse_ref, out_ref, got, got_lse, own, own_sem, send_sem, recv_sem, lsend_sem, lrecv_sem):
    me = lax.axis_index("seq")
    place = ring_place(me, n)
    groups, width = got.shape[2], got.shape[4]
    ways = (1, -1)
    beside = [ring_index(place + way, n) for way in ways]
    barrier = pltpu.get_barrier_semaphore()
    for other in beside:
        pl.semaphore_signal(barrier, inc=1, device_id={"seq": other}, device_id_type=MESH)

    def home(way, step):
        return ring_index(place - ways[way] * (1 + step), n)

    def fetch(way, step):
        return pltpu.make_async_copy(
            o_ref.at[home(way, step) * 2 + way], own.at[way, lax.rem(step, 2)], own_sem.at[way, lax.rem(step, 2)]
        )

    def copies(way, step, g, before):
        at = home(way, step) * 2 + way
        first = before is None
        return (
            pltpu.make_async_remote_copy(
                src_ref=lse_ref.at[at, g] if first else got_lse.at[way, before, g],
                dst_ref=got_lse.at[way, step, g],
                send_sem=lsend_sem.at[way, step, g],
                recv_sem=lrecv_sem.at[way, step, g],
                device_id={"seq": beside[way]},
                device_id_type=MESH,
            ),
            pltpu.make_async_remote_copy(
                src_ref=o_ref.at[at, g] if first else got.at[way, before, g],
                dst_ref=got.at[way, step, g],
                send_sem=send_sem.at[way, step, g],
                recv_sem=recv_sem.at[way, step, g],
                device_id={"seq": beside[way]},
                device_id_type=MESH,
            ),
        )

    def merged(way, step, g):
        for one in copies(way, step - 1, g, step - 1):
            one.wait_recv()
        if g == 0:
            fetch(way, step).wait()
        at = home(way, step) * 2 + way
        shares, lse = merge(got_lse[way, step - 1, g], lse_ref[at, g])
        columns = []
        for r in range(width // DH):
            cols = slice(r * DH, (r + 1) * DH)
            columns.append(
                got[way, step - 1, g, :, cols].astype(jnp.float32) * shares[:, r : r + 1]
                + own[way, lax.rem(step, 2), g, :, cols].astype(jnp.float32) * shares[:, STAT + r : STAT + r + 1]
            )
        return columns, lse

    for way in range(2):
        fetch(way, 1).start()
    pl.semaphore_wait(barrier, 2)
    for g in range(groups):
        for way in range(2):
            for one in copies(way, 0, g, None):
                one.start()

    def one_step(step, carry):
        for way in range(2):
            fetch(way, step + 1).start()
        for g in range(groups):
            for way in range(2):
                columns, lse = merged(way, step, g)
                got_lse[way, step - 1, g] = lse
                for r, value in enumerate(columns):
                    got[way, step - 1, g, :, r * DH : (r + 1) * DH] = value.astype(jnp.bfloat16)
            for way in range(2):
                for one in copies(way, step, g, step - 1):
                    one.start()
        return carry

    lax.fori_loop(1, n - 1, one_step, 0)
    for g in range(groups):
        for way in range(2):
            columns, _ = merged(way, n - 1, g)
            for r, value in enumerate(columns):
                at = g * width + r * DH
                out_ref[way * BLK : (way + 1) * BLK, at : at + DH] = value.astype(jnp.bfloat16)
    for g in range(groups):
        for way in range(2):
            for one in copies(way, 0, g, None):
                one.wait_send()

    def drain(step, carry):
        for g in range(groups):
            for way in range(2):
                for one in copies(way, step, g, step - 1):
                    one.wait_send()
        return carry

    lax.fori_loop(1, n - 1, drain, 0)


def body(
    queries,
    self_keys,
    self_values,
    store_keys,
    store_values,
    kv_slot,
    neighbours,
    counts,
    out_weight,
):
    n = lax.axis_size("seq")
    head_count = lax.axis_size("head")
    local_blocks, degree = neighbours.shape
    local_rows, width = queries.shape
    store_blocks = store_keys.shape[0] // BLK
    all_blocks = local_blocks * n
    kv_here = store_keys.shape[1] // DH
    group_width = (H // KVH) * DH
    rows = (H // KVH) * BLK
    table = jnp.concatenate([neighbours, counts[:, None]], axis=1)
    table = jnp.pad(table, ((0, 8 - local_blocks), (0, 2 * BLK - table.shape[1] - BLK)))
    all_queries, tables = gathered(queries, n, 2, 0, table)
    near = tables[:, :local_blocks, :degree].reshape(all_blocks, degree)
    count = tables[:, :local_blocks, degree].reshape(all_blocks)
    smem = pl.BlockSpec(memory_space=pltpu.SMEM)

    def whole(a):
        return pl.BlockSpec(a.shape, lambda i: (0, 0))

    parts, lse = pl.pallas_call(
        functools.partial(part_kernel, local_blocks, store_blocks),
        grid=(all_blocks,),
        in_specs=[smem, smem, smem, pl.BlockSpec((BLK, width), lambda i: (i, 0))]
        + [whole(a) for a in (self_keys, self_values, store_keys, store_values)],
        out_specs=[
            pl.BlockSpec((1, kv_here, BLK, group_width), lambda i: (i, 0, 0, 0)),
            pl.BlockSpec((1, kv_here, STAT, BLK), lambda i: (i, 0, 0, 0)),
        ],
        out_shape=[
            jax.ShapeDtypeStruct((all_blocks, kv_here, BLK, group_width), jnp.bfloat16),
            jax.ShapeDtypeStruct((all_blocks, kv_here, STAT, BLK), jnp.float32),
        ],
        scratch_shapes=[
            pltpu.SMEM((degree + 1,), jnp.int32),
            pltpu.VMEM((kv_here, rows, DH), jnp.float32),
            pltpu.VMEM((kv_here, rows, BLK), jnp.float32),
            pltpu.VMEM((kv_here, rows, BLK), jnp.float32),
        ],
        compiler_params=pltpu.CompilerParams(vmem_limit_bytes=40 << 20),
        cost_estimate=pl.CostEstimate(flops=2_000_000_000, bytes_accessed=12 << 20, transcendentals=4_000_000),
    )(kv_slot, near, count, all_queries, self_keys, self_values, store_keys, store_values)
    dma = pltpu.SemaphoreType.DMA((2, n - 1, kv_here))
    attended = pl.pallas_call(
        functools.partial(reduce_kernel, n),
        in_specs=[pl.BlockSpec(memory_space=pl.ANY), pl.BlockSpec(memory_space=pltpu.VMEM)],
        out_specs=pl.BlockSpec(memory_space=pltpu.VMEM),
        out_shape=jax.ShapeDtypeStruct((local_rows, width), jnp.bfloat16),
        scratch_shapes=[
            pltpu.VMEM((2, n - 1, kv_here, BLK, group_width), jnp.bfloat16),
            pltpu.VMEM((2, n - 1, kv_here, STAT, BLK), jnp.float32),
            pltpu.VMEM((2, 2, kv_here, BLK, group_width), jnp.bfloat16),
            pltpu.SemaphoreType.DMA((2, 2)),
            dma,
            dma,
            dma,
            dma,
        ],
        compiler_params=pltpu.CompilerParams(
            collective_id=1, has_side_effects=True, vmem_limit_bytes=50 << 20
        ),
    )(parts, lse)
    (all_attended,) = gathered(attended, n, 2, 2)
    partial_value = jnp.dot(all_attended, out_weight, preferred_element_type=jnp.float32).astype(jnp.bfloat16)
    columns = out_weight.shape[1]
    share = local_rows // head_count
    split = partial_value.reshape(n, head_count, share, columns).transpose(1, 0, 2, 3)
    summed = lax.psum_scatter(split.reshape(head_count * n * share, columns), "head", scatter_dimension=0, tiled=True)
    summed = summed.reshape(n, share, columns)
    swapped = lax.all_to_all(summed, "seq", split_axis=0, concat_axis=0, tiled=True)
    return jnp.transpose(swapped, (1, 0, 2)).reshape(share, n * columns)


def solution(mesh):
    placed = (
        P("seq", "head"),
        P("seq", "head"),
        P("seq", "head"),
        P("seq", "head"),
        P("seq", "head"),
        P(),
        P("seq", None),
        P("seq"),
        P("head", "seq"),
    )
    return jax.shard_map(
        body, mesh=mesh, in_specs=placed, out_specs=P(("seq", "head"), None), check_vma=False
    )
```

time: 338 us -> 236 us (0.70)
  waiting for transfers between devices: 166 us -> 30.6 us
  Pallas kernels: 117 us -> 152 us
  local copies, waits for them, and re-layouts: 10.7 us -> 14.3 us
    all_gather x2 -> x0, waiting for transfers between devices: 134 us -> none  [the longest x1 81.5 us: body(): weight = lax.all_gather(out_weight, 'seq', axis=1, tiled=True)]
    pallas_call x1 -> x3, Pallas kernels: 102 us -> 137 us  [the longest x2 90.5 us: gathered(): pl.pallas_call(functools.partial(gather_kernel, n, pieces, with_table), i...]
    all_gather x1 -> x0, blocking collectives: 22.6 us -> none  [body(): lists = lax.all_gather(lists, 'seq', axis=0, tiled=True)]
    all_to_all x0 -> x1, blocking collectives: none -> 19.9 us  [body(): lax.all_to_all(summed, 'seq', split_axis=0, concat_axis=0, tiled=True)]
    unnamed x14 -> x18, local copies, waits for them, and re-layouts: 9.81 us -> 10.8 us
  transfers between devices with their start and end apart: 3 -> 1, of which waited for: 3 -> 1; matrix products, arithmetic and copies ran while one was open for 0% -> 0% of each run, Pallas kernels for 35% -> 0%
where the time goes in v2:
time: 236 us; the launch traced here: 235 us
  Pallas kernels  152 us (64%)
  waiting for transfers between devices  30.6 us (13%)
  blocking collectives  19.9 us (8%)
  local copies, waits for them, and re-layouts  14.3 us (6%)
  between operations  13.5 us (6%)
  matrix products  4.54 us (2%)
    pallas_call x2, Pallas kernels, gathered(): pl.pallas_call(functools.partial(gather_kernel, n, pieces, with_table), i...  90.5 us
    pallas_call x1, Pallas kernels, body(): pl.pallas_call(functools.partial(reduce_kernel, n), in_specs=[pl.BlockSpe...  46.4 us
    reduce_scatter x1, waiting for transfers between devices, body(): lax.psum_scatter(split.reshape(head_count * n * share, columns), 'head',...  30.6 us
    all_to_all x1, blocking collectives, body(): lax.all_to_all(summed, 'seq', split_axis=0, concat_axis=0, tiled=True)  19.9 us
    pallas_call x1, Pallas kernels, body(): pl.pallas_call(functools.partial(part_kernel, local_blocks, store_blocks)...  14.8 us
    unnamed x18, local copies, waits for them, and re-layouts  10.8 us
  transfers between devices with their start and end apart: 1, of which 1 were waited for; matrix products, arithmetic and copies ran while one was open for 0% of the time, Pallas kernels for 0%

profile of v2, /device:TPU:0, one launch (start us, length us, event | category | flops | bytes accessed | tf_op | source)
XLA Modules:
  0.0 235.3 jit_solution(12516527861665904053)
XLA Ops:
  6.5 0.0 copy-start
  6.5 0.8 copy.13
  7.4 0.8 pad_add_fusion
  8.1 1.0 copy-done.5
  9.2 49.3 %shard_map.91 = (bf16[2048,1024]{1,0:T(8,128)(2,1)}, s32[8,8,128]{2,1,0:T(8,128)S(1)}) custom-call(bf16[256,1024]{1,0:T(8,128)(2,1)S(1)} %copy-done.5, s32[8,128]{1,0:T(8,128)S(1)} %pad.4.refs_1_), custom_call_target="tpu_custom_call" | custom-call | tf_op jit(solution)/shard_map/pallas_call | solution.py:221
  58.5 0.3 slice_reduce_fusion
  58.7 0.1 reshape_squeeze.3.count_ref
  58.8 2.2 copy-done.2
  61.0 1.6 copy-done.3
  62.6 1.6 copy-done.4
  64.2 0.9 copy-done.6
  65.1 0.9 copy-done.7
  66.0 0.7 copy-done.8
  66.7 14.8 %shard_map.92 = (bf16[16,2,128,512]{3,2,1,0:T(8,128)(2,1)S(1)}, f32[16,2,8,128]{3,2,1,0:T(8,128)S(1)}) custom-call(s32[256]{0:T(256)S(1)} %copy-done.8, s32[16,64]{1,0:T(8,128)S(1)} %bitcast.12, s32[16]{0:T(128)S(1)} %reshape_squeeze.3.count_ref, bf16[2048,1024]{1,0:T(8,128)(2,1)S(1)} %copy-done.2, bf16[256,256]{1,0:T(8,128)(2,1)S(1)} %copy-done.6, ...), custom_call_target="tpu_custom_call" | custom-call | flops 2000000000 | bytes 12582912 | tf_op jit(solution)/shard_map/pallas_call | solution.py:372
  81.5 0.0 copy-start.1
  81.5 1.9 copy-done.1
  83.4 46.4 %shard_map.93.refs_0_ = bf16[256,1024]{1,0:T(8,128)(2,1)S(1)} custom-call(bf16[16,2,128,512]{3,2,1,0:T(8,128)(2,1)} %copy-done.1, f32[16,2,8,128]{3,2,1,0:T(8,128)S(1)} %get-tuple-element.12.lse_ref), custom_call_target="tpu_custom_call" | custom-call | tf_op jit(solution)/shard_map/pallas_call | solution.py:395
  129.9 41.2 %shard_map.94 = bf16[2048,1024]{1,0:T(8,128)(2,1)} custom-call(bf16[256,1024]{1,0:T(8,128)(2,1)S(1)} %shard_map.93.refs_0_), custom_call_target="tpu_custom_call" | custom-call | tf_op jit(solution)/shard_map/pallas_call | solution.py:221
  171.1 4.5 %convolution_convert_fusion = bf16[2048,512]{1,0:T(8,128)(2,1)S(1)} fusion(bf16[2048,1024]{1,0:T(8,128)(2,1)} %shard_map.94, bf16[1024,512]{1,0:T(8,128)(2,1)S(1)} %copy-done), kind=kOutput, calls=%fused_computation | convolution fusion | flops 2148532224 | bytes 7340032 | tf_op jit(solution)/shard_map/dot_general | solution.py:415
  175.6 1.5 copy.14
  177.1 0.0 reduce-scatter.2.cloned.1.call-update
  177.1 30.6 %reduce-scatter.2.cloned.1.call-done = bf16[512,512]{1,0:T(8,128)(2,1)} async-done(((bf16[2048,512]{1,0:T(8,128)(2,1)}), bf16[512,512]{1,0:T(8,128)(2,1)}) %reduce-scatter.2.cloned.1.call-update) | async-done | bytes 524304 | tf_op jit(solution)/shard_map/reduce_scatter | solution.py:419
  207.7 19.9 %all_to_all.5 = bf16[8,64,512]{2,1,0:T(8,128)(2,1)S(1)} all-to-all(bf16[8,64,512]{2,1,0:T(8,128)(2,1)} %bitcast.16), channel_id=1, replica_groups=mesh['seq'=8,'head'=4] {'seq'}, dimensions={0} | all-to-all | bytes 1048576 | tf_op jit(solution)/shard_map/all_to_all | solution.py:421
  227.6 0.8 copy.16
  (11 shorter events, 0.0 us)
Async XLA Ops:
  6.5 164.5 %copy-start = (bf16[1024,512]{1,0:T(8,128)(2,1)S(1)}, bf16[1024,512]{1,0:T(8,128)(2,1)}, u32[]{:S(2)}) copy-start(bf16[1024,512]{1,0:T(8,128)(2,1)} %param.17) | copy-start | bytes 3145732
  6.5 201.1 %reduce-scatter.2.cloned.1.call-start = ((), (), s32[]{:S(2)}) async-start(), calls=%async_computation.2 | async-start | bytes 2621440 | tf_op jit(solution)/shard_map/reduce_scatter | solution.py:419
  8.1 1.0 copy-start.5
  58.8 2.2 copy-start.2
  61.0 1.6 copy-start.3
  62.6 1.6 copy-start.4
  64.2 0.9 copy-start.6
  65.1 0.9 copy-start.7
  66.0 0.7 copy-start.8
  81.5 1.9 copy-start.1
Sparse Core Ops, SparseCore 0:
  177.3 30.3 reduce-scatter.1

commit v3 on v2

--- a/solution.py
+++ b/solution.py
@@ -337,6 +337,87 @@
         return carry
 
     lax.fori_loop(1, n - 1, drain, 0)
+
+
+def finish_kernel(n, heads, p_ref, out_ref, got, summed, landed, hsend, hrecv, send_sem, recv_sem):
+    me = lax.axis_index("seq")
+    mine = lax.axis_index("head")
+    columns = p_ref.shape[3]
+    barrier = pltpu.get_barrier_semaphore()
+    for k in range(1, heads):
+        pl.semaphore_signal(barrier, inc=1, device_id={"head": lax.rem(mine + k, heads)}, device_id_type=MESH)
+    for k in range(1, n):
+        pl.semaphore_signal(barrier, inc=1, device_id={"seq": lax.rem(me + k, n)}, device_id_type=MESH)
+    pl.semaphore_wait(barrier, heads + n - 2)
+    first = []
+    for k in range(1, heads):
+        to = lax.rem(mine + k, heads)
+        first.append(
+            pltpu.make_async_remote_copy(
+                src_ref=p_ref.at[to],
+                dst_ref=got.at[k],
+                send_sem=hsend.at[k],
+                recv_sem=hrecv.at[k],
+                device_id={"head": to},
+                device_id_type=MESH,
+            )
+        )
+    for one in first:
+        one.start()
+    for one in first:
+        one.wait()
+
+    def add(i, carry):
+        total = p_ref[mine, i].astype(jnp.float32)
+        for k in range(1, heads):
+            total = total + got[k, i].astype(jnp.float32)
+        summed[i] = total.astype(jnp.bfloat16)
+        return carry
+
+    lax.fori_loop(0, n, add, 0)
+    second = []
+    for k in range(1, n):
+        to = lax.rem(me + k, n)
+        second.append(
+            pltpu.make_async_remote_copy(
+                src_ref=summed.at[to],
+                dst_ref=landed.at[me],
+                send_sem=send_sem.at[k],
+                recv_sem=recv_sem.at[k],
+                device_id={"seq": to},
+                device_id_type=MESH,
+            )
+        )
+    for one in second:
+        one.start()
+    landed[me] = summed[me]
+    for one in second:
+        one.wait()
+    for i in range(n):
+        out_ref[:, i * columns : (i + 1) * columns] = landed[i]
+
+
+def finished(split):
+    heads, n, share, columns = split.shape
+    vmem = pl.BlockSpec(memory_space=pltpu.VMEM)
+    return pl.pallas_call(
+        functools.partial(finish_kernel, n, heads),
+        in_specs=[vmem],
+        out_specs=vmem,
+        out_shape=jax.ShapeDtypeStruct((share, n * columns), split.dtype),
+        scratch_shapes=[
+            pltpu.VMEM(split.shape, split.dtype),
+            pltpu.VMEM((n, share, columns), split.dtype),
+            pltpu.VMEM((n, share, columns), split.dtype),
+            pltpu.SemaphoreType.DMA((heads,)),
+            pltpu.SemaphoreType.DMA((heads,)),
+            pltpu.SemaphoreType.DMA((n,)),
+            pltpu.SemaphoreType.DMA((n,)),
+        ],
+        compiler_params=pltpu.CompilerParams(
+            collective_id=3, has_side_effects=True, vmem_limit_bytes=50 << 20
+        ),
+    )(split)
 
 
 def body(
@@ -416,10 +497,7 @@
     columns = out_weight.shape[1]
     share = local_rows // head_count
     split = partial_value.reshape(n, head_count, share, columns).transpose(1, 0, 2, 3)
-    summed = lax.psum_scatter(split.reshape(head_count * n * share, columns), "head", scatter_dimension=0, tiled=True)
-    summed = summed.reshape(n, share, columns)
-    swapped = lax.all_to_all(summed, "seq", split_axis=0, concat_axis=0, tiled=True)
-    return jnp.transpose(swapped, (1, 0, 2)).reshape(share, n * columns)
+    return finished(split)
 
 
 def solution(mesh):

time: 236 us -> 209 us (0.89)
  Pallas kernels: 152 us -> 188 us
  waiting for transfers between devices: 30.6 us -> 0 us
  blocking collectives: 19.9 us -> 0 us
  between operations: 13.5 us -> 0.09 us
    pallas_call x0 -> x1, Pallas kernels: none -> 36 us  [finished(): pl.pallas_call(functools.partial(finish_kernel, n, heads), in_specs=[vmem...]
    reduce_scatter x1 -> x0, waiting for transfers between devices: 30.6 us -> none  [body(): lax.psum_scatter(split.reshape(head_count * n * share, columns), 'head',...]
    all_to_all x1 -> x0, blocking collectives: 19.9 us -> none  [body(): lax.all_to_all(summed, 'seq', split_axis=0, concat_axis=0, tiled=True)]
    pallas_call x1, Pallas kernels: 46.4 us -> 48.9 us  [body(): pl.pallas_call(functools.partial(reduce_kernel, n), in_specs=[pl.BlockSpe...]
    unnamed x18 -> x19, local copies, waits for them, and re-layouts: 10.8 us -> 11.6 us
  transfers between devices with their start and end apart: 1 -> 0, of which waited for: 1 -> 0; matrix products, arithmetic and copies ran while one was open for 0% -> 0% of each run, Pallas kernels for 0% -> 0%
where the time goes in v3:
time: 209 us; the launch traced here: 207 us
  Pallas kernels  188 us (90%)
  local copies, waits for them, and re-layouts  13 us (6%)
  matrix products  4.52 us (2%)
    pallas_call x2, Pallas kernels, gathered(): pl.pallas_call(functools.partial(gather_kernel, n, pieces, with_table), i...  90.5 us
    pallas_call x1, Pallas kernels, body(): pl.pallas_call(functools.partial(reduce_kernel, n), in_specs=[pl.BlockSpe...  48.9 us
    pallas_call x1, Pallas kernels, finished(): pl.pallas_call(functools.partial(finish_kernel, n, heads), in_specs=[vmem...  36 us
    pallas_call x1, Pallas kernels, body(): pl.pallas_call(functools.partial(part_kernel, local_blocks, store_blocks)...  12.9 us
    unnamed x19, local copies, waits for them, and re-layouts  11.6 us
    dot_general x1, matrix products, body(): jnp.dot(all_attended, out_weight, preferred_element_type=jnp.float32)  4.52 us

profile of v3, /device:TPU:0, one launch (start us, length us, event | category | flops | bytes accessed | tf_op | source)
XLA Modules:
  0.0 206.6 jit_solution(15536063896964228319)
XLA Ops:
  0.0 0.0 copy-start
  0.0 0.8 copy.11
  0.8 0.8 pad_add_fusion
  1.6 0.0 copy-start.5
  1.6 1.0 copy-done.5
  2.6 49.3 %shard_map.91 = (bf16[2048,1024]{1,0:T(8,128)(2,1)}, s32[8,8,128]{2,1,0:T(8,128)S(1)}) custom-call(bf16[256,1024]{1,0:T(8,128)(2,1)S(1)} %copy-done.5, s32[8,128]{1,0:T(8,128)S(1)} %pad.4.refs_1_), custom_call_target="tpu_custom_call" | custom-call | tf_op jit(solution)/shard_map/pallas_call | solution.py:221
  51.9 0.3 slice_reduce_fusion
  52.2 0.1 reshape_squeeze.3.count_ref
  52.3 2.2 %copy-done.2 = bf16[2048,1024]{1,0:T(8,128)(2,1)S(1)} copy-done((bf16[2048,1024]{1,0:T(8,128)(2,1)S(1)}, bf16[2048,1024]{1,0:T(8,128)(2,1)}, u32[]{:S(2)}) %copy-start.2) | copy-done | bytes 4194328
  54.5 1.6 copy-done.3
  56.1 1.6 copy-done.4
  57.7 0.9 copy-done.6
  58.6 0.9 copy-done.7
  59.5 0.7 copy-done.8
  60.2 12.9 %shard_map.92 = (bf16[16,2,128,512]{3,2,1,0:T(8,128)(2,1)S(1)}, f32[16,2,8,128]{3,2,1,0:T(8,128)S(1)}) custom-call(s32[256]{0:T(256)S(1)} %copy-done.8, s32[16,64]{1,0:T(8,128)S(1)} %bitcast.9, s32[16]{0:T(128)S(1)} %reshape_squeeze.3.count_ref, bf16[2048,1024]{1,0:T(8,128)(2,1)S(1)} %copy-done.2, bf16[256,256]{1,0:T(8,128)(2,1)S(1)} %copy-done.6, ...), custom_call_target="tpu_custom_call" | custom-call | flops 2000000000 | bytes 12582912 | tf_op jit(solution)/shard_map/pallas_call | solution.py:453
  73.0 0.0 copy-start.1
  73.0 1.9 copy-done.1
  75.0 48.9 %shard_map.93.refs_0_ = bf16[256,1024]{1,0:T(8,128)(2,1)S(1)} custom-call(bf16[16,2,128,512]{3,2,1,0:T(8,128)(2,1)} %copy-done.1, f32[16,2,8,128]{3,2,1,0:T(8,128)S(1)} %get-tuple-element.12.lse_ref), custom_call_target="tpu_custom_call" | custom-call | tf_op jit(solution)/shard_map/pallas_call | solution.py:476
  123.8 41.2 %shard_map.94 = bf16[2048,1024]{1,0:T(8,128)(2,1)} custom-call(bf16[256,1024]{1,0:T(8,128)(2,1)S(1)} %shard_map.93.refs_0_), custom_call_target="tpu_custom_call" | custom-call | tf_op jit(solution)/shard_map/pallas_call | solution.py:221
  165.1 0.0 copy-done
  165.1 4.5 %convolution_convert_fusion = bf16[2048,512]{1,0:T(8,128)(2,1)S(1)} fusion(bf16[2048,1024]{1,0:T(8,128)(2,1)} %shard_map.94, bf16[1024,512]{1,0:T(8,128)(2,1)S(1)} %copy-done), kind=kOutput, calls=%fused_computation | convolution fusion | flops 2148532224 | bytes 7340032 | tf_op jit(solution)/shard_map/dot_general | solution.py:496
  169.6 0.1 copy.14
  169.7 36.0 %shard_map.95 = bf16[64,4096]{1,0:T(8,128)(2,1)S(1)} custom-call(bf16[4,8,64,512]{3,2,1,0:T(8,128)(2,1)S(1)} %bitcast.8), custom_call_target="tpu_custom_call" | custom-call | tf_op jit(solution)/shard_map/pallas_call | solution.py:403
  205.8 0.8 copy.16
  (8 shorter events, 0.0 us)
Async XLA Ops:
  0.0 165.1 %copy-start = (bf16[1024,512]{1,0:T(8,128)(2,1)S(1)}, bf16[1024,512]{1,0:T(8,128)(2,1)}, u32[]{:S(2)}) copy-start(bf16[1024,512]{1,0:T(8,128)(2,1)} %param.17) | copy-start | bytes 3145732
  1.6 1.0 copy-start.5
  52.3 2.2 %copy-start.2 = (bf16[2048,1024]{1,0:T(8,128)(2,1)S(1)}, bf16[2048,1024]{1,0:T(8,128)(2,1)}, u32[]{:S(2)}) copy-start(bf16[2048,1024]{1,0:T(8,128)(2,1)} %get-tuple-element.10.q_ref) | copy-start | bytes 12582916
  54.5 1.6 copy-start.3
  56.1 1.6 copy-start.4
  57.7 0.9 copy-start.6
  58.6 0.9 copy-start.7
  59.5 0.7 copy-start.8
  73.0 1.9 copy-start.1
